TPU v7x, 128 devices: a whole 4x4x4 slice. The times are simulated.
128 devices in a mesh: rep: 1, dp: 128 (over x, y, z, core).
Axes of the slice: x: 4, y: 4, z: 4, core: 2. Of those that a mesh axis runs over, the one named last changes fastest.
Arguments:
- g_w_gate: bfloat16 [128, 2, 640, 2048], P(('rep', 'dp'))
- g_w_up: bfloat16 [128, 2, 640, 2048], P(('rep', 'dp'))
- g_w_down: bfloat16 [128, 2, 2048, 640], P(('rep', 'dp'))
- w_gate: bfloat16 [2, 640, 2048], replicated
- w_up: bfloat16 [2, 640, 2048], replicated
- w_down: bfloat16 [2, 2048, 640], replicated
- m_w_gate: float32 [2, 640, 2048], P(None, 'dp')
- m_w_up: float32 [2, 640, 2048], P(None, 'dp')
- m_w_down: float32 [2, 2048, 640], P(None, 'dp')
- v_w_gate: float32 [2, 640, 2048], P(None, 'dp')
- v_w_up: float32 [2, 640, 2048], P(None, 'dp')
- v_w_down: float32 [2, 2048, 640], P(None, 'dp')
Outputs:
- output 1: bfloat16 [2, 640, 2048], P('rep')
- output 2: bfloat16 [2, 640, 2048], P('rep')
- output 3: bfloat16 [2, 2048, 640], P('rep')
- output 4: float32 [2, 640, 2048], P('rep', 'dp')
- output 5: float32 [2, 640, 2048], P('rep', 'dp')
- output 6: float32 [2, 2048, 640], P('rep', 'dp')
- output 7: float32 [2, 640, 2048], P('rep', 'dp')
- output 8: float32 [2, 640, 2048], P('rep', 'dp')
- output 9: float32 [2, 2048, 640], P('rep', 'dp')
All inputs are finite; a program needn't handle non-finite values.
Results may differ from a plain program's by a relative error of at most 0.022.
Values are sent between devices in bfloat16 or wider.
A program may use at most 1.5 GiB of HBM per device.

v0:
```python
import jax
import jax.numpy as jnp
from jax import lax
from jax.sharding import PartitionSpec as P


def adamw(w, m, v, g):
    m = 0.9 * m + 0.1 * g
    v = 0.95 * v + 0.05 * g * g
    step = m * lax.rsqrt(v + 1e-8) + 0.1 * w
    return (w - 0.02 * step).astype(jnp.bfloat16), m, v


def solution(mesh):
    def step(*arrays):
        terms, weights, m, v = (arrays[i : i + 3] for i in (0, 3, 6, 9))
        gradients = [lax.psum_scatter(t[0], "dp", scatter_dimension=1, tiled=True).astype(jnp.float32) for t in terms]
        me = lax.axis_index("dp")
        own = [lax.dynamic_slice_in_dim(w, me * one.shape[1], one.shape[1], 1).astype(jnp.float32) for w, one in zip(weights, m, strict=True)]
        new = [adamw(w, m, v, g) for w, m, v, g in zip(own, m, v, gradients, strict=True)]
        whole = [lax.all_gather(one[0], "dp", axis=1, tiled=True) for one in new]
        return (*whole, *(one[1] for one in new), *(one[2] for one in new))

    all_of, cut = P(None, None, None), P(None, "dp", None)
    return jax.shard_map(
        step,
        mesh=mesh,
        in_specs=(P(("rep", "dp"), None, None, None),) * 3 + (all_of,) * 3 + (cut,) * 6,
        out_specs=(P("rep", None, None),) * 3 + (P("rep", "dp", None),) * 6,
        check_vma=False,
    )
```

profile of v0, /device:TPU:1, one launch (start us, length us, event | category | flops | bytes accessed | tf_op | source)
XLA Modules:
  0.0 1062.5 jit_solution(5828448304167161678)
XLA Ops:
  7.2 0.0 all-reduce.5.cloned.1.call-start
  7.2 20.0 %copy_bitcast_fusion = (bf16[2,640,2048]{2,0,1:T(2,128)(2,1)}, bf16[2,640,2048]{2,0,1:T(2,128)(2,1)}) fusion(bf16[1,2,640,2048]{3,2,1,0:T(8,128)(2,1)} %param.13, bf16[1,2,640,2048]{3,2,1,0:T(8,128)(2,1)} %param.12), kind=kLoop, calls=%fused_computation | loop fusion | bytes 20971520 | tf_op jit(solution)/shard_map/squeeze | solution.py:17
  27.3 0.0 all-reduce.5.cloned.1.call-update
  27.3 0.0 copy-start
  27.3 0.0 copy-start.1
  27.3 0.0 copy-start.2
  27.3 0.0 copy-start.3
  27.3 0.0 copy-start.4
  27.3 0.0 copy-start.5
  27.4 0.0 reduce-scatter.2.cloned.1.call-start
  27.4 0.7 reduce-scatter.2.cloned.1.call-update
  28.1 0.0 all-gather.6.cloned.1.call-start
  28.2 1.0 constant_dynamic-slice_fusion
  29.2 166.0 %all-reduce.5.cloned.1.call-done = (bf16[2,640,2048]{2,0,1:T(2,128)(2,1)}, bf16[2,640,2048]{2,0,1:T(2,128)(2,1)}) async-done(((bf16[2,640,2048]{2,0,1:T(2,128)(2,1)}, bf16[2,640,2048]{2,0,1:T(2,128)(2,1)}), (bf16[2,640,2048]{2,0,1:T(2,128)(2,1)}, bf16[2,640,2048]{2,0,1:T(2,128)(2,1)})) %all-reduce.5.cloned.1.call-update) | async-done | bytes 10485776
  195.2 0.0 copy-done
  195.2 0.0 copy-done.1
  195.2 1.7 fusion.14
  196.9 0.0 all-gather.6.cloned.1.call-update
  196.9 0.0 all-gather.4.cloned.1.call-start
  197.0 0.0 copy-done.2
  197.0 1.7 fusion.13
  198.7 0.0 all-gather.4.cloned.1.call-update
  198.7 0.0 all-gather.8.cloned.1.call-start
  198.7 643.0 %reduce-scatter.2.cloned.1.call-done = bf16[2,16,640]{2,1,0:T(8,128)(2,1)} async-done(((bf16[2,2048,640]{2,1,0:T(8,128)(2,1)}), bf16[2,16,640]{2,1,0:T(8,128)(2,1)}) %reduce-scatter.2.cloned.1.call-update) | async-done | bytes 40976 | tf_op jit(solution)/shard_map/reduce_scatter | solution.py:17
  841.8 1.5 fusion.8
  843.3 0.0 all-gather.8.cloned.1.call-update
  843.3 70.5 %all-gather.6.cloned.1.call-done = bf16[2,640,2048]{2,0,1:T(2,128)(2,1)} async-done(((bf16[2,5,2048]{2,0,1:T(2,128)(2,1)}), bf16[2,640,2048]{2,0,1:T(2,128)(2,1)}) %all-gather.6.cloned.1.call-update) | async-done | bytes 5242896 | tf_op jit(solution)/shard_map/all_gather | solution.py:21
  913.8 7.2 copy.32
  921.1 61.4 %all-gather.4.cloned.1.call-done = bf16[2,640,2048]{2,0,1:T(2,128)(2,1)} async-done(((bf16[2,5,2048]{2,0,1:T(2,128)(2,1)}), bf16[2,640,2048]{2,0,1:T(2,128)(2,1)}) %all-gather.4.cloned.1.call-update) | async-done | bytes 5242896 | tf_op jit(solution)/shard_map/all_gather | solution.py:21
  982.5 7.2 copy.31
  989.7 61.0 %all-gather.8.cloned.1.call-done = bf16[2,2048,640]{2,1,0:T(8,128)(2,1)} async-done(((bf16[2,16,640]{2,1,0:T(8,128)(2,1)}), bf16[2,2048,640]{2,1,0:T(8,128)(2,1)}) %all-gather.8.cloned.1.call-update) | async-done | bytes 5242896 | tf_op jit(solution)/shard_map/all_gather | solution.py:21
  1050.7 5.3 copy.42
  (3 shorter events, 0.0 us)
Async XLA Ops:
  7.2 188.1 %all-reduce.5.cloned.1.call-start = ((), (), s32[]{:S(2)}) async-start(), calls=%async_computation.5 | async-start | bytes 20971520
  27.3 167.9 %copy-start = (f32[2,5,2048]{2,0,1:T(2,128)S(1)}, f32[2,5,2048]{2,0,1:T(2,128)}, u32[]{:S(2)}) copy-start(f32[2,5,2048]{2,0,1:T(2,128)} %param.22) | copy-start | bytes 245764
  27.3 167.9 %copy-start.1 = (f32[2,5,2048]{2,0,1:T(2,128)S(1)}, f32[2,5,2048]{2,0,1:T(2,128)}, u32[]{:S(2)}) copy-start(f32[2,5,2048]{2,0,1:T(2,128)} %param.19) | copy-start | bytes 245764
  27.3 169.7 %copy-start.2 = (f32[2,5,2048]{2,0,1:T(2,128)S(1)}, f32[2,5,2048]{2,0,1:T(2,128)}, u32[]{:S(2)}) copy-start(f32[2,5,2048]{2,0,1:T(2,128)} %param.21) | copy-start | bytes 245764
  27.3 169.7 %copy-start.3 = (f32[2,5,2048]{2,0,1:T(2,128)S(1)}, f32[2,5,2048]{2,0,1:T(2,128)}, u32[]{:S(2)}) copy-start(f32[2,5,2048]{2,0,1:T(2,128)} %param.18) | copy-start | bytes 245764
  27.3 814.4 %copy-start.4 = (f32[2,16,640]{2,1,0:T(8,128)S(1)}, f32[2,16,640]{2,1,0:T(8,128)}, u32[]{:S(2)}) copy-start(f32[2,16,640]{2,1,0:T(8,128)} %param.23) | copy-start | bytes 245764
  27.3 814.4 %copy-start.5 = (f32[2,16,640]{2,1,0:T(8,128)S(1)}, f32[2,16,640]{2,1,0:T(8,128)}, u32[]{:S(2)}) copy-start(f32[2,16,640]{2,1,0:T(8,128)} %param.20) | copy-start | bytes 245764
  27.4 814.4 %reduce-scatter.2.cloned.1.call-start = ((), (), s32[]{:S(2)}) async-start(), calls=%async_computation.3 | async-start | bytes 5283840 | tf_op jit(solution)/shard_map/reduce_scatter | solution.py:17
  28.1 885.7 %all-gather.6.cloned.1.call-start = ((), (), s32[]{:S(2)}) async-start(), calls=%async_computation.2 | async-start | bytes 5283840 | tf_op jit(solution)/shard_map/all_gather | solution.py:21
  196.9 785.5 %all-gather.4.cloned.1.call-start = ((), (), s32[]{:S(2)}) async-start(), calls=%async_computation.1 | async-start | bytes 5283840 | tf_op jit(solution)/shard_map/all_gather | solution.py:21
  198.7 852.0 %all-gather.8.cloned.1.call-start = ((), (), s32[]{:S(2)}) async-start(), calls=%async_computation.4 | async-start | bytes 5283840 | tf_op jit(solution)/shard_map/all_gather | solution.py:21
Sparse Core Ops, SparseCore 0:
  27.4 167.7 all-reduce.4
  197.6 644.1 reduce-scatter.1
  845.3 68.4 all-gather.5
  917.2 65.1 all-gather.3
  985.5 65.1 all-gather.7
where the time goes:
time: 1060 us
  waiting for transfers between devices  1000 us (94%)
  local copies, waits for them, and re-layouts  40.8 us (4%)
  between operations  13.9 us (1%)
    reduce_scatter x1, waiting for transfers between devices, step(): lax.psum_scatter(t[0], 'dp', scatter_dimension=1, tiled=True)  643 us
    all_gather x3, waiting for transfers between devices, step(): whole = [lax.all_gather(one[0], 'dp', axis=1, tiled=True) for one in new]  193 us
    unnamed x6, waiting for transfers between devices  167 us
  transfers between devices with their start and end apart: 5, of which 5 were waited for; matrix products, arithmetic and copies ran while one was open for 2% of the time, Pallas kernels for 0%

commit v1 on v0

v1 whole, which is shorter than its diff:
```python
import jax
import jax.numpy as jnp
from jax import lax
from jax.experimental import pallas as pl
from jax.experimental.pallas import tpu as pltpu
from jax.sharding import PartitionSpec as P

F32, BF16 = jnp.float32, jnp.bfloat16
MESH = pl.DeviceIdType.MESH
COPIES = 224
WIDE, TALL = (2, 4, 4, 5, 2, 64, 128), (2, 4, 4, 4, 2, 80, 128)
HALF = ((2, 4, 4, 5, 64, 128), (2, 4, 4, 5, 64, 128), (2, 4, 4, 4, 80, 128))
SHARD = (
    ((4, 5, 64, 128), (5, 64, 128), (5, 16, 128)),
    ((4, 5, 64, 128), (4, 5, 16, 128), (5, 16, 128)),
    ((4, 4, 80, 128), (4, 80, 128), (80, 128)),
)
AXES = (("x", "y", "z"), ("y", "z", "x"), ("z", "x", "y"))
SMALL = ((5, 32, 128), (5, 32, 128), (2, 80, 128))


def adamw(w, m, v, g):
    m = 0.9 * m + 0.1 * g
    v = 0.95 * v + 0.05 * g * g
    step = m * lax.rsqrt(v + 1e-8) + 0.1 * w
    return w - 0.02 * step, m, v


def add_into(dst, *others):
    def at(index):
        total = dst[index].astype(F32)
        for one in others:
            total = total + one[index].astype(F32)
        dst[index] = total.astype(BF16)

    lead = dst.shape[:-2]
    if len(lead) < 2:
        for i in range(lead[0] if lead else 1):
            at((i,) if lead else ())
        return

    @pl.loop(0, lead[0])
    def _(i):
        for j in range(lead[1]):
            at((i, j))


def kernel(*refs):
    grads, weights, ms, vs = (refs[i : i + 3] for i in (0, 3, 6, 9))
    outs, new_ms, new_vs = (refs[i : i + 3] for i in (12, 15, 18))
    own, other, gathered = (refs[i : i + 3] for i in (21, 24, 27))
    landing = (refs[30:33], refs[33:36], refs[36:39])
    m_in, v_in = refs[39:42], refs[42:45]
    rows, w_block, w_down, turned, out_box, in_box, back_out, back_in, send_sems, recv_sems, local_sems = refs[45:]

    me = lax.axis_index("dp")
    core = lax.rem(me, 2)
    pos = {"z": lax.rem(me // 2, 4), "y": lax.rem(me // 8, 4), "x": me // 32}
    d = 2 * pos["z"] + core

    def device(core=core, **moved):
        at = {**pos, **moved}
        return ((at["x"] * 4 + at["y"]) * 4 + at["z"]) * 2 + core

    def step(axis, by):
        return lax.rem(pos[axis] + by + 4, 4)

    partner = device(core=1 - core)
    right = {a: device(**{a: step(a, 1)}) for a in "xyz"}
    left = {a: device(**{a: step(a, -1)}) for a in "xyz"}
    line = [lax.rem(d + k, 8) for k in range(1, 8)]
    line_device = [device(core=lax.rem(t, 2), z=t // 2) for t in line]

    used = [0, 0]
    sent = []

    def send(src, dst, to):
        copy = pltpu.make_async_remote_copy(
            src_ref=src,
            dst_ref=dst,
            send_sem=send_sems.at[used[0]],
            recv_sem=recv_sems.at[used[0]],
            device_id={"dp": to},
            device_id_type=MESH,
        )
        used[0] += 1
        copy.start()
        sent.append(copy)
        return copy

    def local(src, dst):
        copy = pltpu.make_async_copy(src, dst, local_sems.at[used[1]])
        used[1] += 1
        copy.start()
        return copy

    def of_whole(ref, weight, layer, s, side):
        if weight == 0:
            return ref.at[layer, s, :, :, side]
        if weight == 1:
            return ref.at[layer, :, s, :, side]
        return ref.at[layer, :, :, s, side]

    def part(ref, weight, phase, layer, s):
        if phase == 0:
            return ref.at[layer, s]
        first = pos[AXES[weight][0]]
        if weight == 0:
            z = pl.ds(pl.multiple_of(16 * s, 16), 16)
            return ref.at[layer, first, s] if phase == 1 else ref.at[layer, first, pos["y"], :, z]
        if weight == 1:
            z = pl.ds(pl.multiple_of(16 * (s if phase == 1 else pos["z"]), 16), 16)
            return ref.at[layer, first, :, :, z] if phase == 1 else ref.at[layer, first, s, :, z]
        return ref.at[layer, first, s] if phase == 1 else ref.at[layer, first, pos["x"], s]

    order = (((2, 0), (2, 1)), ((1, 1), (-1, 0)), ((1, 0), (-1, 1)), ((0, 0), (0, 1)))
    loads = {}
    for group in order:
        for by, layer in group:
            for weight in range(3):
                s = step(AXES[weight][0], by)
                loads[weight, by, layer] = local(of_whole(grads[weight], weight, layer, s, core), own[weight].at[layer, s])
    x, y, z = pos["x"], pos["y"], pos["z"]
    small = [local(ms[i], m_in[i]) for i in range(3)] + [local(vs[i], v_in[i]) for i in range(3)]
    small += [local(weights[i].at[:, x, y], w_block.at[i]) for i in range(2)]
    small += [local(weights[2].at[:, x, y, z, core], w_down)]

    barrier = pltpu.get_barrier_semaphore()
    peers = [right["x"], left["x"], right["y"], left["y"], *line_device]
    for peer in peers:
        pl.semaphore_signal(barrier, inc=1, device_id={"dp": peer}, device_id_type=MESH)
    pl.semaphore_wait(barrier, len(peers))

    pairs = {}
    for group in order:
        for by, layer in group:
            for weight in range(3):
                s = step(AXES[weight][0], by)
                pairs[weight, by, layer] = send(
                    of_whole(grads[weight], weight, layer, s, 1 - core), other[weight].at[layer, s], partner
                )

    def pair_sum(weight, by, layer, *more):
        loads[weight, by, layer].wait()
        pairs[weight, by, layer].wait_recv()
        s = step(AXES[weight][0], by)
        add_into(own[weight].at[layer, s], other[weight].at[layer, s], *more)

    for phase in range(3):
        first, raw, summed = {}, {}, {}

        def shard(weight, by, layer, phase=phase):
            return part(own[weight], weight, phase, layer, step(AXES[weight][phase], by))

        def land(weight, which, layer, phase=phase):
            return landing[phase][weight].at[which, layer]

        def ways(weight, phase=phase):
            axis = AXES[weight][phase]
            return right[axis], left[axis]

        for weight in range(3):
            for layer in range(2):
                if phase == 0:
                    pair_sum(weight, 2, layer)
                first[weight, layer] = send(shard(weight, 2, layer), land(weight, 0, layer), ways(weight)[layer])
        for weight in range(3):
            for layer, by in ((1, 1), (0, -1)):
                if phase == 0:
                    pair_sum(weight, by, layer)
                raw[weight, layer] = send(shard(weight, by, layer), land(weight, 1, layer), ways(weight)[1 - layer])
        if phase == 0:
            for weight in range(3):
                for layer, by in ((0, 1), (1, -1)):
                    pair_sum(weight, by, layer)
        for weight in range(3):
            for layer, by in ((0, 1), (1, -1)):
                first[weight, layer].wait_recv()
                add_into(shard(weight, by, layer), land(weight, 0, layer))
                summed[weight, layer] = send(shard(weight, by, layer), land(weight, 2, layer), ways(weight)[layer])
        if phase == 0:
            for weight in range(3):
                for layer in range(2):
                    pair_sum(weight, 0, layer)
        if phase == 1:
            for one in small:
                one.wait()
            for weight in range(2):
                for layer in range(2):

                    @pl.loop(0, 5)
                    def _(i, weight=weight, layer=layer):
                        for side in range(2):
                            block = w_block[weight, layer, i, side].astype(F32)
                            for t in range(8):
                                start = 256 * i + 2 * (8 * side + t) + layer
                                turned[weight, pl.ds(start, 8, 32), :] = block[8 * t : 8 * t + 8]
        for weight in range(3):
            for layer in range(2):
                raw[weight, layer].wait_recv()
                summed[weight, layer].wait_recv()
                add_into(shard(weight, 0, layer), land(weight, 1, layer), land(weight, 2, layer))

    for weight in range(2):
        for layer in range(2):
            block = part(own[weight], weight, 2, layer, pos[AXES[weight][2]])
            for i in range(5):
                both = block[i].astype(F32)
                for t in range(2):
                    rows[pl.ds(64 * i + 4 * weight + 2 * t + layer, 8, 8), :] = both[8 * t : 8 * t + 8]
    for t in range(8):
        out_box[t] = rows[40 * t : 40 * t + 40].reshape(5, 8, 128).astype(BF16)
    moves = [send(out_box.at[t], in_box.at[d], to) for t, to in zip(line, line_device)]
    in_box[d] = out_box[d]

    for layer in range(2):
        g = part(own[2], 2, 2, layer, pos["y"])[...].astype(F32)
        w, m, v = adamw(w_down[layer].astype(F32), m_in[2][layer], v_in[2][layer], g)
        m_in[2][layer] = m
        v_in[2][layer] = v
        gathered[2][layer, pos["z"], pos["x"], pos["y"]] = w.astype(BF16)

    for one in moves:
        one.wait_recv()
    low = lax.broadcasted_iota(jnp.int32, (8, 128), 0) < 4

    def swap(a, b):
        return jnp.where(low, a, pltpu.roll(b, 4, 0)), jnp.where(low, pltpu.roll(a, 4, 0), b)

    for side in range(2):
        for half in range(2):
            even, odd = 4 * half + side, 4 * half + 2 + side

            @pl.loop(0, 5)
            def _(r, side=side, half=half, even=even, odd=odd):
                new = []
                at = 8 * (2 * side + half)
                gs = swap(in_box[even, r].astype(F32), in_box[odd, r].astype(F32))
                for weight in range(2):
                    here = (r, pl.ds(at, 8))
                    w = turned[weight, pl.ds(pl.multiple_of(160 * d + 32 * r + at, 8), 8), :]
                    w, m, v = adamw(w, m_in[weight][here], v_in[weight][here], gs[weight])
                    m_in[weight][here] = m
                    v_in[weight][here] = v
                    new.append(w)
                to_even, to_odd = swap(*new)
                back_out[even, r] = to_even.astype(BF16)
                back_out[odd, r] = to_odd.astype(BF16)

    moves = [send(back_out.at[t], back_in.at[d], to) for t, to in zip(line, line_device)]
    back_in[d] = back_out[d]
    results = [local(m_in[i], new_ms[i]) for i in range(3)] + [local(v_in[i], new_vs[i]) for i in range(3)]
    for one in moves:
        one.wait_recv()
    for t in range(8):
        rows[40 * t : 40 * t + 40] = back_in[t].astype(F32).reshape(40, 128)
    for weight in range(2):
        for layer in range(2):
            block = part(gathered[weight], weight, 2, layer, pos[AXES[weight][2]])
            for i in range(5):
                both = [rows[pl.ds(64 * i + 4 * weight + 2 * t + layer, 8, 8), :] for t in range(2)]
                block[i] = jnp.concatenate(both, 0).astype(BF16)

    arrivals = []
    for phase in (2, 1, 0):
        firsts, lasts, forwards = {}, {}, {}

        def shard(weight, by, layer, phase=phase):
            return part(gathered[weight], weight, phase, layer, step(AXES[weight][phase], by))

        def spread(weight, by, layer, phase=phase):
            if phase == 0:
                s = step(AXES[weight][0], by)
                src = gathered[weight].at[layer, s]
                dst = of_whole(outs[weight], weight, layer, s, core)
                arrivals.append(send(src, dst, partner))
                results.append(local(src, dst))

        for weight in range(3):
            axis = AXES[weight][phase]
            for layer in range(2):
                firsts[weight, layer] = send(shard(weight, 0, layer), shard(weight, 0, layer), (right[axis], left[axis])[layer])
        for weight in range(3):
            axis = AXES[weight][phase]
            for layer in range(2):
                lasts[weight, layer] = send(shard(weight, 0, layer), shard(weight, 0, layer), (left[axis], right[axis])[layer])
        for weight in range(3):
            for layer in range(2):
                spread(weight, 0, layer)
        for weight in range(3):
            axis = AXES[weight][phase]
            for layer, by in ((0, -1), (1, 1)):
                firsts[weight, layer].wait_recv()
                forwards[weight, layer] = send(shard(weight, by, layer), shard(weight, by, layer), (right[axis], left[axis])[layer])
                spread(weight, by, layer)
        for weight in range(3):
            for layer, by in ((0, 1), (1, -1)):
                lasts[weight, layer].wait_recv()
                spread(weight, by, layer)
        for weight in range(3):
            for layer in range(2):
                forwards[weight, layer].wait_recv()
                spread(weight, 2, layer)

    for one in results:
        one.wait()
    for one in arrivals:
        one.wait_recv()
    for one in sent:
        one.wait_send()


def wide(a):
    return a.reshape(2, 80, 8, 16, 128).transpose(0, 1, 3, 2, 4).reshape(WIDE)


def tall(a):
    return a.reshape(2, 256, 8, 5, 128).transpose(0, 1, 3, 2, 4).reshape(TALL)


def wide_small(a):
    return a.transpose(1, 0, 2).reshape(5, 2, 16, 128).transpose(0, 2, 1, 3).reshape(5, 32, 128)


def tall_small(a):
    return a.reshape(2, 2, 8, 5, 128).transpose(0, 1, 3, 2, 4).reshape(2, 80, 128)


def unwide(a):
    return a.reshape(2, 80, 16, 8, 128).transpose(0, 1, 3, 2, 4).reshape(2, 640, 2048)


def untall(a):
    return a.reshape(2, 256, 5, 8, 128).transpose(0, 1, 3, 2, 4).reshape(2, 2048, 640)


def unwide_small(a):
    return a.reshape(5, 16, 2, 128).transpose(0, 2, 1, 3).reshape(5, 2, 2048).transpose(1, 0, 2)


def untall_small(a):
    return a.reshape(2, 2, 5, 8, 128).transpose(0, 1, 3, 2, 4).reshape(2, 16, 640)


def solution(mesh):
    def step(*arrays):
        big, small = (wide, wide, tall), (wide_small, wide_small, tall_small)
        operands = [f(a[0]) for f, a in zip(big, arrays[:3])] + [f(a) for f, a in zip(big, arrays[3:6])]
        operands += [f(a) for f, a in zip(small * 2, arrays[6:])]
        shapes = (WIDE, WIDE, TALL)
        landing = [pltpu.VMEM((3, 2, *SHARD[weight][phase]), BF16) for phase in range(3) for weight in range(3)]
        new = pl.pallas_call(
            kernel,
            name="step",
            out_shape=[jax.ShapeDtypeStruct(s, BF16) for s in shapes] + [jax.ShapeDtypeStruct(s, F32) for s in SMALL * 2],
            in_specs=[pl.BlockSpec(memory_space=pl.ANY)] * 12,
            out_specs=[pl.BlockSpec(memory_space=pl.ANY)] * 9,
            scratch_shapes=[
                *[pltpu.VMEM(s, BF16) for s in HALF * 3],
                *landing,
                *[pltpu.VMEM(s, F32) for s in SMALL * 2],
                pltpu.VMEM((320, 128), F32),
                pltpu.VMEM((2, 2, 5, 2, 64, 128), BF16),
                pltpu.VMEM((2, 80, 128), BF16),
                pltpu.VMEM((2, 1280, 128), F32),
                *[pltpu.VMEM((8, 5, 8, 128), BF16)] * 4,
                pltpu.SemaphoreType.DMA((COPIES,)),
                pltpu.SemaphoreType.DMA((COPIES,)),
                pltpu.SemaphoreType.DMA((80,)),
            ],
            compiler_params=pltpu.CompilerParams(
                collective_id=0, has_side_effects=True, vmem_limit_bytes=44 * 1024 * 1024
            ),
        )(*operands)
        back, small_back = (unwide, unwide, untall), (unwide_small, unwide_small, untall_small)
        return tuple(f(a) for f, a in zip(back + small_back * 2, new))

    all_of, cut = P(None, None, None), P(None, "dp", None)
    return jax.shard_map(
        step,
        mesh=mesh,
        in_specs=(P(("rep", "dp"), None, None, None),) * 3 + (all_of,) * 3 + (cut,) * 6,
        out_specs=(P("rep", None, None),) * 3 + (P("rep", "dp", None),) * 6,
        check_vma=False,
    )
```

time: 1060 us -> 125 us (0.12)
  waiting for transfers between devices: 1000 us -> 0 us
  Pallas kernels: 0 us -> 105 us
  local copies, waits for them, and re-layouts: 40.8 us -> 18.9 us
  between operations: 13.9 us -> 0.69 us
    reduce_scatter x1 -> x0, waiting for transfers between devices: 643 us -> none  [step(): lax.psum_scatter(t[0], 'dp', scatter_dimension=1, tiled=True)]
    all_gather x3 -> x0, waiting for transfers between devices: 193 us -> none  [step(): whole = [lax.all_gather(one[0], 'dp', axis=1, tiled=True) for one in new]]
    unnamed x6 -> x0, waiting for transfers between devices: 167 us -> none
    pallas_call x0 -> x1, Pallas kernels: none -> 105 us  [step(): pl.pallas_call(kernel, name='step', out_shape=[jax.ShapeDtypeStruct(s, BF...]
    squeeze x1 -> x0, local copies, waits for them, and re-layouts: 20 us -> none  [step(): t[0]]
  transfers between devices with their start and end apart: 5 -> 0, of which waited for: 5 -> 0; matrix products, arithmetic and copies ran while one was open for 2% -> 0% of each run, Pallas kernels for 0% -> 0%
where the time goes in v1:
time: 125 us; the launch traced here: 124 us
  Pallas kernels  105 us (84%)
  local copies, waits for them, and re-layouts  18.9 us (15%)
    pallas_call x1, Pallas kernels, step(): pl.pallas_call(kernel, name='step', out_shape=[jax.ShapeDtypeStruct(s, BF...  105 us
    unnamed x27, local copies, waits for them, and re-layouts  18.9 us

profile of v1, /device:TPU:1, one launch (start us, length us, event | category | flops | bytes accessed | tf_op | source)
XLA Modules:
  0.0 124.3 jit_solution(9162266279103953223)
XLA Ops:
  0.6 0.0 copy-start
  0.7 0.9 copy-done
  1.5 0.0 copy-start.1
  1.5 0.9 copy-done.1
  2.4 0.0 copy-start.2
  2.4 0.9 copy-done.2
  3.3 0.0 copy-start.3
  3.3 0.9 copy-done.3
  4.2 0.0 copy-start.4
  4.2 0.9 copy-done.4
  5.1 0.0 copy-start.5
  5.1 0.9 copy-done.5
  6.0 104.7 %step.1 = (bf16[2,4,4,5,2,64,128]{6,5,4,3,2,1,0:T(8,128)(2,1)S(1)}, bf16[2,4,4,5,2,64,128]{6,5,4,3,2,1,0:T(8,128)(2,1)}, bf16[2,4,4,4,2,80,128]{6,5,4,3,2,1,0:T(...) custom-call(bf16[2,4,4,5,2,64,128]{6,5,4,3,2,1,0:T(8,128)(2,1)} %bit, ...), custom_call_target="tpu_custom_call" | custom-call | tf_op jit(solution)/shard_map/step/pallas_call | solution.py:352
  110.6 0.0 copy-start.6
  110.6 0.0 slice-start
  110.7 2.7 %copy.34 = bf16[2,640,2048]{2,1,0:T(8,128)(2,1)} copy(bf16[2,640,2048]{2,1,0:T(8,128)(2,1)S(1)} %bitcast.121) | data formatting | bytes 10485760
  113.3 1.7 %copy-done.6 = bf16[2,4,4,5,2,64,128]{6,5,4,3,2,1,0:T(8,128)(2,1)S(1)} copy-done((bf16[2,4,4,5,2,64,128]{6,5,4,3,2,1,0:T(8,128)(2,1)S(1)}, bf16[2,4,4,5,2,64,128]{6,5,4,3,2,1,0:T(8,128)(2,1)}, u32[]{:S(2)}) %copy-start.6) | copy-done | bytes 5242904
  115.0 0.0 slice-start.1
  115.0 2.4 %copy.35 = bf16[2,640,2048]{2,1,0:T(8,128)(2,1)} copy(bf16[2,640,2048]{2,1,0:T(8,128)(2,1)S(1)} %bitcast.143) | data formatting | bytes 10485760
  117.4 0.0 slice-done
  117.4 0.6 slice-done.1
  118.1 2.4 %copy.36 = bf16[2,2048,640]{2,1,0:T(8,128)(2,1)} copy(bf16[2,2048,640]{2,1,0:T(8,128)(2,1)S(1)} %bitcast.142) | data formatting | bytes 10485760
  120.4 0.6 copy.37
  121.1 0.6 copy.38
  121.7 0.6 copy.39
  122.3 0.6 copy.40
  123.0 0.6 copy.41
  123.6 0.6 copy.42
  (1 shorter events, 0.0 us)
Async XLA Ops:
  0.6 0.9 copy-start
  1.5 0.9 copy-start.1
  2.4 0.9 copy-start.2
  3.3 0.9 copy-start.3
  4.2 0.9 copy-start.4
  5.1 0.9 copy-start.5
  110.6 4.4 %copy-start.6 = (bf16[2,4,4,5,2,64,128]{6,5,4,3,2,1,0:T(8,128)(2,1)S(1)}, bf16[2,4,4,5,2,64,128]{6,5,4,3,2,1,0:T(8,128)(2,1)}, u32[]{:S(2)}) copy-start(bf16[2,4,4,5,2,64,128]{6,5,4,3,2,1,0:T(8,128)(2,1)} %get-tuple-element.19) | copy-start | bytes 15728644
  110.6 6.8 %slice-start = ((s8[5242880]{0:T(1024)(128)(4,1)}), s8[4194304]{0:T(1024)(128)(4,1)S(1)}, s32[]{:S(2)}) async-start(s8[5242880]{0:T(1024)(128)(4,1)} %bitcast.140), calls=%async_computation | async-start | bytes 8388608
  115.0 3.1 %slice-start.1 = ((s8[5242880]{0:T(1024)(128)(4,1)}), s8[1048576]{0:T(1024)(128)(4,1)S(1)}, s32[]{:S(2)}) async-start(s8[5242880]{0:T(1024)(128)(4,1)} %bitcast.140), calls=%async_computation.1 | async-start | bytes 2097152

commit v2 on v1

--- a/solution.py
+++ b/solution.py
@@ -48,15 +48,16 @@
 def kernel(*refs):
     grads, weights, ms, vs = (refs[i : i + 3] for i in (0, 3, 6, 9))
     outs, new_ms, new_vs = (refs[i : i + 3] for i in (12, 15, 18))
-    own, other, gathered = (refs[i : i + 3] for i in (21, 24, 27))
-    landing = (refs[30:33], refs[33:36], refs[36:39])
-    m_in, v_in = refs[39:42], refs[42:45]
-    rows, w_block, w_down, turned, out_box, in_box, back_out, back_in, send_sems, recv_sems, local_sems = refs[45:]
+    own, other = (refs[i : i + 3] for i in (21, 24))
+    landing = (refs[27:30], refs[30:33], refs[33:36])
+    m_in, v_in = refs[36:39], refs[39:42]
+    rows, w_block, w_down, turned, out_box, in_box, back_out, back_in, send_sems, recv_sems, local_sems = refs[42:]
 
     me = lax.axis_index("dp")
     core = lax.rem(me, 2)
     pos = {"z": lax.rem(me // 2, 4), "y": lax.rem(me // 8, 4), "x": me // 32}
-    d = 2 * pos["z"] + core
+    x, y, z = pos["x"], pos["y"], pos["z"]
+    d = 2 * z + core
 
     def device(core=core, **moved):
         at = {**pos, **moved}
@@ -113,6 +114,17 @@
             return ref.at[layer, first, :, :, z] if phase == 1 else ref.at[layer, first, s, :, z]
         return ref.at[layer, first, s] if phase == 1 else ref.at[layer, first, pos["x"], s]
 
+    def part_of_whole(ref, weight, phase, layer, s):
+        if phase == 0:
+            return of_whole(ref, weight, layer, s, core)
+        if weight == 0:
+            rows_of_z = pl.ds(pl.multiple_of(16 * s, 16), 16)
+            return ref.at[layer, x, s, :, core] if phase == 1 else ref.at[layer, x, y, :, core, rows_of_z]
+        if weight == 1:
+            rows_of_z = pl.ds(pl.multiple_of(16 * (s if phase == 1 else z), 16), 16)
+            return ref.at[layer, :, y, :, core, rows_of_z] if phase == 1 else ref.at[layer, s, y, :, core, rows_of_z]
+        return ref.at[layer, s, :, z, core] if phase == 1 else ref.at[layer, x, s, z, core]
+
     order = (((2, 0), (2, 1)), ((1, 1), (-1, 0)), ((1, 0), (-1, 1)), ((0, 0), (0, 1)))
     loads = {}
     for group in order:
@@ -120,7 +132,6 @@
             for weight in range(3):
                 s = step(AXES[weight][0], by)
                 loads[weight, by, layer] = local(of_whole(grads[weight], weight, layer, s, core), own[weight].at[layer, s])
-    x, y, z = pos["x"], pos["y"], pos["z"]
     small = [local(ms[i], m_in[i]) for i in range(3)] + [local(vs[i], v_in[i]) for i in range(3)]
     small += [local(weights[i].at[:, x, y], w_block.at[i]) for i in range(2)]
     small += [local(weights[2].at[:, x, y, z, core], w_down)]
@@ -216,9 +227,9 @@
     for layer in range(2):
         g = part(own[2], 2, 2, layer, pos["y"])[...].astype(F32)
         w, m, v = adamw(w_down[layer].astype(F32), m_in[2][layer], v_in[2][layer], g)
-        m_in[2][layer] = m
-        v_in[2][layer] = v
-        gathered[2][layer, pos["z"], pos["x"], pos["y"]] = w.astype(BF16)
+        new_ms[2][layer] = m
+        new_vs[2][layer] = v
+        outs[2][layer, x, y, z, core] = w.astype(BF16)
 
     for one in moves:
         one.wait_recv()
@@ -240,8 +251,8 @@
                     here = (r, pl.ds(at, 8))
                     w = turned[weight, pl.ds(pl.multiple_of(160 * d + 32 * r + at, 8), 8), :]
                     w, m, v = adamw(w, m_in[weight][here], v_in[weight][here], gs[weight])
-                    m_in[weight][here] = m
-                    v_in[weight][here] = v
+                    new_ms[weight][here] = m
+                    new_vs[weight][here] = v
                     new.append(w)
                 to_even, to_odd = swap(*new)
                 back_out[even, r] = to_even.astype(BF16)
@@ -249,14 +260,13 @@
 
     moves = [send(back_out.at[t], back_in.at[d], to) for t, to in zip(line, line_device)]
     back_in[d] = back_out[d]
-    results = [local(m_in[i], new_ms[i]) for i in range(3)] + [local(v_in[i], new_vs[i]) for i in range(3)]
     for one in moves:
         one.wait_recv()
     for t in range(8):
         rows[40 * t : 40 * t + 40] = back_in[t].astype(F32).reshape(40, 128)
     for weight in range(2):
         for layer in range(2):
-            block = part(gathered[weight], weight, 2, layer, pos[AXES[weight][2]])
+            block = part_of_whole(outs[weight], weight, 2, layer, pos[AXES[weight][2]])
             for i in range(5):
                 both = [rows[pl.ds(64 * i + 4 * weight + 2 * t + layer, 8, 8), :] for t in range(2)]
                 block[i] = jnp.concatenate(both, 0).astype(BF16)
@@ -266,15 +276,11 @@
         firsts, lasts, forwards = {}, {}, {}
 
         def shard(weight, by, layer, phase=phase):
-            return part(gathered[weight], weight, phase, layer, step(AXES[weight][phase], by))
+            return part_of_whole(outs[weight], weight, phase, layer, step(AXES[weight][phase], by))
 
         def spread(weight, by, layer, phase=phase):
             if phase == 0:
-                s = step(AXES[weight][0], by)
-                src = gathered[weight].at[layer, s]
-                dst = of_whole(outs[weight], weight, layer, s, core)
-                arrivals.append(send(src, dst, partner))
-                results.append(local(src, dst))
+                arrivals.append(send(shard(weight, by, layer), shard(weight, by, layer), partner))
 
         for weight in range(3):
             axis = AXES[weight][phase]
@@ -302,12 +308,22 @@
                 forwards[weight, layer].wait_recv()
                 spread(weight, 2, layer)
 
-    for one in results:
-        one.wait()
     for one in arrivals:
         one.wait_recv()
     for one in sent:
         one.wait_send()
+
+
+def write_out(*refs):
+    copies, sems = [], refs[-1]
+    for src, dst in zip(refs[:9], refs[9:18]):
+        parts = [(i, j) for i in range(2) for j in range(4)] if len(src.shape) == 7 else [()]
+        for at in parts:
+            src_at, dst_at = (src.at[at], dst.at[at]) if at else (src, dst)
+            copies.append(pltpu.make_async_copy(src_at, dst_at, sems.at[len(copies)]))
+            copies[-1].start()
+    for one in copies:
+        one.wait()
 
 
 def wide(a):
@@ -349,14 +365,15 @@
         operands += [f(a) for f, a in zip(small * 2, arrays[6:])]
         shapes = (WIDE, WIDE, TALL)
         landing = [pltpu.VMEM((3, 2, *SHARD[weight][phase]), BF16) for phase in range(3) for weight in range(3)]
+        results = [(s, BF16) for s in shapes] + [(s, F32) for s in SMALL * 2]
         new = pl.pallas_call(
             kernel,
             name="step",
-            out_shape=[jax.ShapeDtypeStruct(s, BF16) for s in shapes] + [jax.ShapeDtypeStruct(s, F32) for s in SMALL * 2],
-            in_specs=[pl.BlockSpec(memory_space=pl.ANY)] * 12,
-            out_specs=[pl.BlockSpec(memory_space=pl.ANY)] * 9,
+            out_shape=[pltpu.VMEM(s, t) for s, t in results],
+            in_specs=[pl.BlockSpec(memory_space=pltpu.HBM)] * 12,
+            out_specs=[pl.BlockSpec(memory_space=pltpu.VMEM)] * 9,
             scratch_shapes=[
-                *[pltpu.VMEM(s, BF16) for s in HALF * 3],
+                *[pltpu.VMEM(s, BF16) for s in HALF * 2],
                 *landing,
                 *[pltpu.VMEM(s, F32) for s in SMALL * 2],
                 pltpu.VMEM((320, 128), F32),
@@ -372,6 +389,15 @@
                 collective_id=0, has_side_effects=True, vmem_limit_bytes=44 * 1024 * 1024
             ),
         )(*operands)
+        new = pl.pallas_call(
+            write_out,
+            name="write_out",
+            out_shape=[jax.ShapeDtypeStruct(s, t) for s, t in results],
+            in_specs=[pl.BlockSpec(memory_space=pl.ANY)] * 9,
+            out_specs=[pl.BlockSpec(memory_space=pltpu.HBM)] * 9,
+            scratch_shapes=[pltpu.SemaphoreType.DMA((30,))],
+            compiler_params=pltpu.CompilerParams(vmem_limit_bytes=1024 * 1024),
+        )(*new)
         back, small_back = (unwide, unwide, untall), (unwide_small, unwide_small, untall_small)
         return tuple(f(a) for f, a in zip(back + small_back * 2, new))
 

time: 125 us -> 111 us (0.89)
  local copies, waits for them, and re-layouts: 18.9 us -> 0 us
  Pallas kernels: 105 us -> 110 us
    unnamed x27 -> x0, local copies, waits for them, and re-layouts: 18.9 us -> none
    pallas_call x1 -> x2, Pallas kernels: 105 us -> 110 us  [the longest x1 104 us: step(): pl.pallas_call(kernel, name='step', out_shape=[pltpu.VMEM(s, t) for s, t...]
where the time goes in v2:
time: 111 us
  Pallas kernels  110 us (99%)
    pallas_call x1, Pallas kernels, step(): pl.pallas_call(kernel, name='step', out_shape=[pltpu.VMEM(s, t) for s, t...  104 us
    pallas_call x1, Pallas kernels, step(): pl.pallas_call(write_out, name='write_out', out_shape=[jax.ShapeDtypeStru...  5.89 us

profile of v2, /device:TPU:1, one launch (start us, length us, event | category | flops | bytes accessed | tf_op | source)
XLA Modules:
  0.0 110.7 jit_solution(2148561522477957957)
XLA Ops:
  0.6 104.2 %step.1 = (bf16[2,4,4,5,2,64,128]{6,5,4,3,2,1,0:T(8,128)(2,1)S(1)}, bf16[2,4,4,5,2,64,128]{6,5,4,3,2,1,0:T(8,128)(2,1)S(1)}, bf16[2,4,4,4,2,80,128]{6,5,4,3,2,1,...) custom-call(bf16[2,4,4,5,2,64,128]{6,5,4,3,2,1,0:T(8,128)(2,1)} %bit, ...), custom_call_target="tpu_custom_call" | custom-call | tf_op jit(solution)/shard_map/step/pallas_call | solution.py:369
  104.9 5.9 %write_out.1 = (bf16[2,4,4,5,2,64,128]{6,5,4,3,2,1,0:T(8,128)(2,1)}, bf16[2,4,4,5,2,64,128]{6,5,4,3,2,1,0:T(8,128)(2,1)}, bf16[2,4,4,4,2,80,128]{6,5,4,3,2,1,0:T...) custom-call(bf16[2,4,4,5,2,64,128]{6,5,4,3,2,1,0:T(8,128)(2,1)S(1)} , ...), custom_call_target="tpu_custom_call" | custom-call | tf_op jit(solution)/shard_map/write_out/pallas_call | solution.py:392

commit v3 on v0

v3 whole, which is shorter than its diff:
```python
import jax
import jax.numpy as jnp
from jax import lax
from jax.experimental import pallas as pl
from jax.experimental.pallas import tpu as pltpu
from jax.sharding import PartitionSpec as P

F32, BF16 = jnp.float32, jnp.bfloat16
MESH = pl.DeviceIdType.MESH
ALL = slice(None)
ROW = 128
WIDE, TALL = (2, 4, 4, 5, 2, 64, ROW), (2, 4, 4, 4, 2, 80, ROW)
HALF = (*[(2, 4, 4, 5, 64, ROW)] * 2, (2, 4, 4, 4, 80, ROW))
AXES = (("xyz", "xyz"), ("yxz", "yxz"), ("zxy", "zyx"))
CUT = (("yz", "yz"), ("xz", "xz"), ("xy", "xx"))
PIECE = ((*[(2, 5, 64, ROW)] * 2, (2, 4, 80, ROW)), (*[(5, 32, ROW)] * 2, (2, 80, ROW)))
SMALL = (*[(160, ROW)] * 2, (2, 80, ROW))
BOX = (2, 5, 8, ROW)
SENDS, RECVS, LOCALS, LAG = 110, 160, 28, 14
ORDER = (
    "A0 R0 O0 B0",
    "W0 A1 C0 R1",
    "O1 W1 D0 B1",
    "E0 C1 H0 D1",
    "J0 E1 K0 H1",
    "L0 J1 Q0 M0",
    "K1 L1 Q1 N0",
    "M1 N1",
)


def adamw(w, m, v, g):
    m = 0.9 * m + 0.1 * g
    v = 0.95 * v + 0.05 * g * g
    step = m * lax.rsqrt(v + 1e-8) + 0.1 * w
    return w - 0.02 * step, m, v


def add_into(dst, *others):
    def at(*index):
        total = dst[index].astype(F32)
        for one in others:
            total = total + one[index].astype(F32)
        dst[index] = total.astype(BF16)

    lead = dst.shape[:-2]
    if not lead:
        at()
    elif len(lead) == 1:
        for i in range(lead[0]):
            at(i)
    else:

        @pl.loop(0, lead[0])
        def _(i):
            for j in range(lead[1]):
                at(i, j)


def kernel(*refs):
    refs = list(refs)

    def take(n):
        taken = refs[:n]
        del refs[:n]
        return taken

    grads, weights, ms, vs, outs, new_ms, new_vs, own, other, *landing, m_in, v_in = (take(3) for _ in range(13))
    last_landing = refs.pop(0)
    w_block, w_down, turned, spread, out_box, in_box, back_out, back_in, send_sems, recv_sems, local_sems = refs

    me = lax.axis_index("dp")
    core = lax.rem(me, 2)
    pos = {"z": lax.rem(lax.div(me, 2), 4), "y": lax.rem(lax.div(me, 8), 4), "x": lax.div(me, 32)}
    x, y, z = (pos[a] for a in "xyz")
    d = 2 * z + core

    stride = {"x": 32, "y": 8, "z": 2}
    steps = {(a, by): lax.rem(pos[a] + by, 4) if by else pos[a] for a in "xyz" for by in (0, 1, 2, 3)}
    devices = {(a, by): me + stride[a] * (steps[a, by] - pos[a]) for a in "xyz" for by in (1, 2, 3)}
    z_rows = [pl.multiple_of(16 * steps["z", by], 16) for by in range(4)]

    def step(axis, by):
        return steps[axis, by % 4]

    def to(axis, by):
        return devices[axis, by % 4]

    partner = me + 1 - 2 * core
    line = [lax.rem(d + i, 8) for i in range(1, 8)]
    line_device = [me - d + t for t in line]
    locals_ = []

    copies, leaving, free_sends, used = {}, [[]], list(range(SENDS)), [0]

    def recycle(stages=LAG):
        leaving.append([])
        for copy, n in (one for old in leaving[:-stages] for one in old):
            copy.wait_send()
            free_sends.append(n)
        del leaving[:-stages]

    def send(src, dst, device_id, key, recv_sem=None):
        if recv_sem is None:
            recv_sem = used[0]
            used[0] += 1
        n = free_sends.pop(0)
        copy = pltpu.make_async_remote_copy(
            src_ref=src,
            dst_ref=dst,
            send_sem=send_sems.at[n],
            recv_sem=recv_sems.at[recv_sem],
            device_id={"dp": device_id},
            device_id_type=MESH,
        )
        copy.start()
        leaving[-1].append((copy, n))
        copies.setdefault(key, []).append(copy)
        return recv_sem

    def arrived(*key):
        for copy in copies[key]:
            copy.wait_recv()

    recv_of = {}

    def local(src, dst, *key):
        copy = pltpu.make_async_copy(src, dst, local_sems.at[len(locals_)])
        copy.start()
        locals_.append(copy)
        return copy

    def spot(w, phase, k, by, half):
        at = {}
        for p, axis in enumerate(AXES[w][k]):
            at[axis] = pos[axis] if p < phase else step(axis, by) if p == phase else ALL
        p = AXES[w][k].index("z")
        rows = ALL if p > phase else pl.ds(z_rows[by % 4 if p == phase else 0], 16)
        if half is not None:
            at[CUT[w][k][phase]] = pl.ds(2 * half, 2)
            if CUT[w][k][phase] == "z":
                rows = pl.ds(32 * half, 32)
        return at["x"], at["y"], at["z"], rows

    def mine(w, phase, k, by, half=None):
        sx, sy, sz, rows = spot(w, phase, k, by, half)
        if w == 2:
            return own[w].at[k, sz, sx, sy]
        first, second = (sx, sy) if w == 0 else (sy, sx)
        return own[w].at[k, first, second, :, rows]

    def whole(ref, w, phase, k, by, half=None, side=core):
        sx, sy, sz, rows = spot(w, phase, k, by, half)
        return ref.at[k, sx, sy, sz, side] if w == 2 else ref.at[k, sx, sy, :, side, rows]

    shards = (2, 1, -1, 0)
    loads = {}
    for k in range(2):
        for by in shards:
            for w in range(3):
                if w == 0 and by == 2:
                    loads[w, k, by] = local(grads[w].at[k, :, :, :, core], own[w].at[k], w, k, by)
                elif w:
                    loads[w, k, by] = local(whole(grads[w], w, 0, k, by), mine(w, 0, k, by), w, k, by)
    small = []
    for w in range(3):
        small += [local(ms[w], m_in[w], "m", w), local(vs[w], v_in[w], "v", w)]
    for w in range(2):
        small += [local(weights[w].at[:, x, y], w_block.at[w], "w", w)]
    small += [local(weights[2].at[:, x, y, z, core], w_down, "w", 2)]

    barrier = pltpu.get_barrier_semaphore()
    peers = [to("x", 1), to("x", -1), to("y", 1), to("y", -1), *line_device]
    for peer in peers:
        pl.semaphore_signal(barrier, inc=1, device_id={"dp": peer}, device_id_type=MESH)
    pl.semaphore_wait(barrier, len(peers))
    for k in range(2):
        for by in shards:
            for w in range(3):
                src = whole(grads[w], w, 0, k, by, side=1 - core)
                send(src, other[w].at[k, step(AXES[w][0][0], by)], partner, ("pair", w, k, by))

    def pair_sum(w, k, by):
        if w or by == 2:
            loads[w, k, by].wait()
        there = other[w].at[k, step(AXES[w][0][0], by)]
        arrived("pair", w, k, by)
        add_into(mine(w, 0, k, by), there)

    def reduce_send(w, p, k, by, which, half, way):
        key = ("r", w, p, k, 2) if which else ("r", w, p, k, 0, half)
        dst = landing[p][w].at[k, which, half]
        recv_of[w, p, k, which, half] = send(mine(w, p, k, by, half), dst, to(AXES[w][k][p], way), key)

    def open_phase(w, p, k, before=lambda w, k, by: None):
        before(w, k, 2)
        for half, way in ((0, 1), (1, -1)):
            reduce_send(w, p, k, 2, 0, half, way)

    def raw_phase(w, p, k, before=lambda w, k, by: None):
        for half, by in ((1, 1), (0, -1)):
            before(w, k, by)
            reduce_send(w, p, k, by, 1, half, by)

    def meet(w, p, k):
        for half, by in ((0, 1), (1, -1)):
            arrived("r", w, p, k, 0, half)
            add_into(mine(w, p, k, by, half), landing[p][w].at[k, 0, half])
            reduce_send(w, p, k, by, 2, half, by)

    def close(w, p, k):
        arrived("r", w, p, k, 2)
        for half in range(2):
            add_into(mine(w, p, k, 0, half), landing[p][w].at[k, 1, half], landing[p][w].at[k, 2, half])

    def stage_a(k):
        for w in range(3):
            open_phase(w, 0, k, pair_sum)

    def stage_r(k):
        for w in range(3):
            raw_phase(w, 0, k, pair_sum)

    def stage_o(k):
        for w in range(3):
            pair_sum(w, k, 0)

    def stage_b(k):
        for w in range(3):
            meet(w, 0, k)

    def stage_c(k):
        for w in range(3):
            close(w, 0, k)
            open_phase(w, 1, k)
            raw_phase(w, 1, k)

    def stage_d(k):
        for w in range(3):
            meet(w, 1, k)

    def to_line(src, dst, *key):
        for t, device_id in zip(line, line_device):
            send(src(t), dst, device_id, key)

    def stage_e(k):
        for w in range(3):
            close(w, 1, k)
            if w == 2:
                for i, by in enumerate((2, 1, -1)):
                    send(mine(w, 2, k, by), last_landing.at[k, i], to(AXES[w][k][2], by), ("r", w, 2, k))

        @pl.loop(0, 5)
        def _(i):
            for w in range(2):
                block = own[w][k, pos[AXES[w][k][0]], pos[AXES[w][k][1]], i].astype(F32)
                for t in range(8):
                    spread[w, pl.ds(64 * i + t, 8, 8), :] = block[8 * t : 8 * t + 8]

        for t in range(8):
            for w in range(2):
                out_box[k, t, w] = spread[w, 40 * t : 40 * t + 40].reshape(5, 8, ROW).astype(BF16)
        to_line(lambda t: out_box.at[k, t], in_box.at[k, d], "out", k)
        in_box[k, d] = out_box[k, d]

    def stage_h(k):
        arrived("out", k)

        @pl.loop(0, 5)
        def _(r):
            for side in range(2):
                for w in range(2):
                    g = in_box[k, side, w, r].astype(F32)
                    for t in range(1, 4):
                        g = g + in_box[k, 2 * t + side, w, r].astype(F32)
                    g = g.astype(BF16).astype(F32)
                    here = pl.ds(32 * r + 16 * side + k, 8, 2)
                    old = turned[w, k, pl.ds(pl.multiple_of(80 * d + 16 * r + 8 * side, 8), 8), :]
                    new, new_ms[w][here, :], new_vs[w][here, :] = adamw(old, m_in[w][here, :], v_in[w][here, :], g)
                    back_out[k, side, w, r] = new.astype(BF16)

        to_line(lambda t: back_out.at[k, lax.rem(t, 2)], back_in.at[k, d], "back", k)
        back_in[k, d] = back_out[k, core]
        arrived("r", 2, 2, k)
        block = mine(2, 2, k, 0)
        add_into(block, *(last_landing.at[k, i] for i in range(3)))
        new, new_ms[2][k], new_vs[2][k] = adamw(w_down[k].astype(F32), m_in[2][k], v_in[2][k], block[...].astype(F32))
        here = whole(outs[2], 2, 2, k, 0)
        here[...] = new.astype(BF16)
        for by in (2, 1, -1):
            send(here, here, to(AXES[2][k][2], by), ("g", 2, 2, k))

    def pass_on(w, p, k, by, half, way, key):
        here = whole(outs[w], w, p, k, by, half)
        which = 2 if key == 3 else 1 if key == 2 else 0
        recv_sem = None if p else recv_of[w, 0, k, which, half]
        send(here, here, to(AXES[w][k][p], way), ("g", w, p, k, key), recv_sem)

    def to_partner(w, k, by):
        here = whole(outs[w], w, 0, k, by)
        send(here, here, partner, ("end", w), (4 * k + shards.index(by)) * 3 + w)

    def open_gather(w, p, k):
        for half, way in ((0, 1), (1, -1)):
            pass_on(w, p, k, 0, half, way, half)

    def open_whole(w, k):
        for key, way in ((0, 1), (1, -1)):
            pass_on(w, 1, k, 0, None, way, key)

    def rest_gather(w, p, k):
        for half, way in ((1, 1), (0, -1)):
            pass_on(w, p, k, 0, half, way, 2)

    def forward(w, p, k):
        for half, way in ((0, 1), (1, -1)):
            arrived("g", w, p, k, half)
            pass_on(w, p, k, -way, half, way, 3)

    def stage_j(k):
        arrived("back", k)
        for w in range(2):
            for t in range(8):
                spread[w, 40 * t : 40 * t + 40] = back_in[k, t, w].astype(F32).reshape(40, ROW)

        @pl.loop(0, 5)
        def _(i):
            for w in range(2):
                tiles = [spread[w, pl.ds(64 * i + t, 8, 8), :] for t in range(8)]
                outs[w][k, x, y, i, core] = jnp.concatenate(tiles, 0).astype(BF16)

        for w in range(2):
            open_whole(w, k)
        arrived("g", 2, 2, k)
        open_whole(2, k)

    def stage_k(k):
        for w in range(3):
            forward(w, 1, k)

    def stage_l(k):
        for w in range(3):
            arrived("g", w, 1, k, 3)
            open_gather(w, 0, k)

    def stage_q(k):
        for w in range(3):
            rest_gather(w, 0, k)
            to_partner(w, k, 0)

    def stage_m(k):
        for w in range(3):
            forward(w, 0, k)

    def stage_n(k):
        for w in range(3):
            arrived("g", w, 0, k, 2)
            for by in (-1, 1):
                to_partner(w, k, by)
        for w in range(3):
            arrived("g", w, 0, k, 3)
            to_partner(w, k, 2)

    def stage_w(k):
        if k == 0:
            for one in small:
                one.wait()

        @pl.loop(0, 5)
        def _(i):
            for w in range(2):
                for side in range(2):
                    block = w_block[w, k, i, side].astype(F32)
                    for t in range(8):
                        turned[w, k, pl.ds(128 * i + 8 * side + t, 8, 16), :] = block[8 * t : 8 * t + 8]

    stages = {n[6:]: f for n, f in locals().items() if n.startswith("stage_")}
    for name in " ".join(ORDER).lower().split():
        recycle()
        stages[name[0]](int(name[1]))

    for w in range(3):
        arrived("end", w)
    for copy, _ in (one for old in leaving for one in old):
        copy.wait_send()


def write_out(*refs):
    copies, sems = [], refs[-1]
    for src, dst in zip(refs[:9], refs[9:18]):
        for at in [(i, j) for i in range(2) for j in range(4)] if len(src.shape) == 7 else [(ALL,)]:
            copies.append(pltpu.make_async_copy(src.at[at], dst.at[at], sems.at[len(copies)]))
            copies[-1].start()
    for one in copies:
        one.wait()


SWAP = (0, 1, 3, 2, 4)


def wide(a):
    return a.reshape(2, 80, 8, 16, ROW).transpose(SWAP).reshape(WIDE)


def tall(a):
    return a.reshape(2, 256, 8, 5, ROW).transpose(SWAP).reshape(TALL)


def wide_small(a):
    return a.reshape(2, 5, 16, ROW).transpose(1, 2, 0, 3).reshape(SMALL[0])


def tall_small(a):
    return a.reshape(2, 2, 8, 5, ROW).transpose(SWAP).reshape(SMALL[2])


def unwide(a):
    return a.reshape(2, 80, 16, 8, ROW).transpose(SWAP).reshape(2, 640, 2048)


def untall(a):
    return a.reshape(2, 256, 5, 8, ROW).transpose(SWAP).reshape(2, 2048, 640)


def unwide_small(a):
    return a.reshape(5, 16, 2, ROW).transpose(2, 0, 1, 3).reshape(2, 5, 2048)


def untall_small(a):
    return a.reshape(2, 2, 5, 8, ROW).transpose(SWAP).reshape(2, 16, 640)


def solution(mesh):
    def step(*arrays):
        big, small = (wide, wide, tall), (wide_small, wide_small, tall_small)
        operands = [f(a[0]) for f, a in zip(big, arrays)] + [f(a) for f, a in zip(big + small * 2, arrays[3:])]
        results = [(s, BF16) for s in (WIDE, WIDE, TALL)] + [(s, F32) for s in SMALL * 2]
        new = pl.pallas_call(
            kernel,
            name="step",
            out_shape=[pltpu.VMEM(s, t) for s, t in results],
            in_specs=[pl.BlockSpec(memory_space=pltpu.HBM)] * 12,
            out_specs=[pl.BlockSpec(memory_space=pltpu.VMEM)] * 9,
            scratch_shapes=[
                *[pltpu.VMEM(s, BF16) for s in HALF * 2],
                *[pltpu.VMEM((2, 3, 2, *s), BF16) for p in PIECE for s in p],
                *[pltpu.VMEM(s, F32) for s in SMALL * 2],
                pltpu.VMEM((2, 3, 80, ROW), BF16),
                pltpu.VMEM((2, 2, 5, 2, 64, ROW), BF16),
                pltpu.VMEM(SMALL[2], BF16),
                pltpu.VMEM((2, 2, 640, ROW), F32),
                pltpu.VMEM((2, 320, ROW), F32),
                *[pltpu.VMEM((2, n, *BOX), BF16) for n in (8, 8, 2, 8)],
                *[pltpu.SemaphoreType.DMA((n,)) for n in (SENDS, RECVS, LOCALS)],
            ],
            compiler_params=pltpu.CompilerParams(collective_id=0, has_side_effects=True, vmem_limit_bytes=44 << 20),
        )(*operands)
        new = pl.pallas_call(
            write_out,
            name="write_out",
            out_shape=[jax.ShapeDtypeStruct(s, t) for s, t in results],
            in_specs=[pl.BlockSpec(memory_space=pl.ANY)] * 9,
            out_specs=[pl.BlockSpec(memory_space=pltpu.HBM)] * 9,
            scratch_shapes=[pltpu.SemaphoreType.DMA((30,))],
            compiler_params=pltpu.CompilerParams(vmem_limit_bytes=1 << 20),
        )(*new)
        back, small_back = (unwide, unwide, untall), (unwide_small, unwide_small, untall_small)
        return tuple(f(a) for f, a in zip(back + small_back * 2, new))

    all_of, cut = P(None, None, None), P(None, "dp", None)
    return jax.shard_map(
        step,
        mesh=mesh,
        in_specs=(P(("rep", "dp"), None, None, None),) * 3 + (all_of,) * 3 + (cut,) * 6,
        out_specs=(P("rep", None, None),) * 3 + (P("rep", "dp", None),) * 6,
        check_vma=False,
    )
```

time: 1060 us -> 95.9 us (0.09)
  waiting for transfers between devices: 1000 us -> 0 us
  Pallas kernels: 0 us -> 95.2 us
  local copies, waits for them, and re-layouts: 40.8 us -> 0 us
  between operations: 13.9 us -> 0.65 us
    reduce_scatter x1 -> x0, waiting for transfers between devices: 643 us -> none  [step(): lax.psum_scatter(t[0], 'dp', scatter_dimension=1, tiled=True)]
    all_gather x3 -> x0, waiting for transfers between devices: 193 us -> none  [step(): whole = [lax.all_gather(one[0], 'dp', axis=1, tiled=True) for one in new]]
    unnamed x6 -> x0, waiting for transfers between devices: 167 us -> none
    pallas_call x0 -> x2, Pallas kernels: none -> 95.2 us  [the longest x1 89.3 us: step(): pl.pallas_call(kernel, name='step', out_shape=[pltpu.VMEM(s, t) for s, t...]
    squeeze x1 -> x0, local copies, waits for them, and re-layouts: 20 us -> none  [step(): t[0]]
    unnamed x15 -> x0, local copies, waits for them, and re-layouts: 19.8 us -> none
  transfers between devices with their start and end apart: 5 -> 0, of which waited for: 5 -> 0; matrix products, arithmetic and copies ran while one was open for 2% -> 0% of each run, Pallas kernels for 0% -> 0%
where the time goes in v3:
time: 95.9 us; the launch traced here: 95.8 us
  Pallas kernels  95.2 us (99%)
    pallas_call x1, Pallas kernels, step(): pl.pallas_call(kernel, name='step', out_shape=[pltpu.VMEM(s, t) for s, t...  89.3 us
    pallas_call x1, Pallas kernels, step(): pl.pallas_call(write_out, name='write_out', out_shape=[jax.ShapeDtypeStru...  5.89 us

profile of v3, /device:TPU:1, one launch (start us, length us, event | category | flops | bytes accessed | tf_op | source)
XLA Modules:
  0.0 95.8 jit_solution(6853623516541430517)
XLA Ops:
  0.6 89.3 %step.1 = (bf16[2,4,4,5,2,64,128]{6,5,4,3,2,1,0:T(8,128)(2,1)S(1)}, bf16[2,4,4,5,2,64,128]{6,5,4,3,2,1,0:T(8,128)(2,1)S(1)}, bf16[2,4,4,4,2,80,128]{6,5,4,3,2,1,...) custom-call(bf16[2,4,4,5,2,64,128]{6,5,4,3,2,1,0:T(8,128)(2,1)} %bit, ...), custom_call_target="tpu_custom_call" | custom-call | tf_op jit(solution)/shard_map/step/pallas_call | solution.py:438
  89.9 5.9 %write_out.1 = (bf16[2,4,4,5,2,64,128]{6,5,4,3,2,1,0:T(8,128)(2,1)}, bf16[2,4,4,5,2,64,128]{6,5,4,3,2,1,0:T(8,128)(2,1)}, bf16[2,4,4,4,2,80,128]{6,5,4,3,2,1,0:T...) custom-call(bf16[2,4,4,5,2,64,128]{6,5,4,3,2,1,0:T(8,128)(2,1)S(1)} , ...), custom_call_target="tpu_custom_call" | custom-call | tf_op jit(solution)/shard_map/write_out/pallas_call | solution.py:458

commit v4 on v3

--- a/solution.py
+++ b/solution.py
@@ -16,15 +16,15 @@
 PIECE = ((*[(2, 5, 64, ROW)] * 2, (2, 4, 80, ROW)), (*[(5, 32, ROW)] * 2, (2, 80, ROW)))
 SMALL = (*[(160, ROW)] * 2, (2, 80, ROW))
 BOX = (2, 5, 8, ROW)
-SENDS, RECVS, LOCALS, LAG = 110, 160, 28, 14
+SENDS, RECVS, LOCALS, LAG = 70, 160, 28, 8
 ORDER = (
     "A0 R0 O0 B0",
     "W0 A1 C0 R1",
     "O1 W1 D0 B1",
     "E0 C1 H0 D1",
     "J0 E1 K0 H1",
-    "L0 J1 Q0 M0",
-    "K1 L1 Q1 N0",
+    "L0 Q0 J1 K1",
+    "M0 L1 Q1 N0",
     "M1 N1",
 )
 
@@ -375,10 +375,11 @@
                         turned[w, k, pl.ds(128 * i + 8 * side + t, 8, 16), :] = block[8 * t : 8 * t + 8]
 
     stages = {n[6:]: f for n, f in locals().items() if n.startswith("stage_")}
-    for name in " ".join(ORDER).lower().split():
-        recycle()
+    for i, name in enumerate(" ".join(ORDER).lower().split()):
+        recycle(LAG if i < 27 else LAG // 2)
         stages[name[0]](int(name[1]))
 
+    recycle(2)
     for w in range(3):
         arrived("end", w)
     for copy, _ in (one for old in leaving for one in old):

time: 95.9 us -> 93.8 us (0.978)
  Pallas kernels: 95.2 us -> 93 us
    pallas_call x1, Pallas kernels: 89.3 us -> 87.1 us  [step(): pl.pallas_call(kernel, name='step', out_shape=[pltpu.VMEM(s, t) for s, t...]
where the time goes in v4:
time: 93.8 us; the launch traced here: 93.7 us
  Pallas kernels  93 us (99%)
    pallas_call x1, Pallas kernels, step(): pl.pallas_call(kernel, name='step', out_shape=[pltpu.VMEM(s, t) for s, t...  87.1 us
    pallas_call x1, Pallas kernels, step(): pl.pallas_call(write_out, name='write_out', out_shape=[jax.ShapeDtypeStru...  5.89 us

profile of v4, /device:TPU:1, one launch (start us, length us, event | category | flops | bytes accessed | tf_op | source)
XLA Modules:
  0.0 93.7 jit_solution(1663688306960160634)
XLA Ops:
  0.6 87.1 %step.1 = (bf16[2,4,4,5,2,64,128]{6,5,4,3,2,1,0:T(8,128)(2,1)S(1)}, bf16[2,4,4,5,2,64,128]{6,5,4,3,2,1,0:T(8,128)(2,1)S(1)}, bf16[2,4,4,4,2,80,128]{6,5,4,3,2,1,...) custom-call(bf16[2,4,4,5,2,64,128]{6,5,4,3,2,1,0:T(8,128)(2,1)} %bit, ...), custom_call_target="tpu_custom_call" | custom-call | tf_op jit(solution)/shard_map/step/pallas_call | solution.py:439
  87.8 5.9 %write_out.1 = (bf16[2,4,4,5,2,64,128]{6,5,4,3,2,1,0:T(8,128)(2,1)}, bf16[2,4,4,5,2,64,128]{6,5,4,3,2,1,0:T(8,128)(2,1)}, bf16[2,4,4,4,2,80,128]{6,5,4,3,2,1,0:T...) custom-call(bf16[2,4,4,5,2,64,128]{6,5,4,3,2,1,0:T(8,128)(2,1)S(1)} , ...), custom_call_target="tpu_custom_call" | custom-call | tf_op jit(solution)/shard_map/write_out/pallas_call | solution.py:459

commit v5 on v4

--- a/solution.py
+++ b/solution.py
@@ -16,14 +16,15 @@
 PIECE = ((*[(2, 5, 64, ROW)] * 2, (2, 4, 80, ROW)), (*[(5, 32, ROW)] * 2, (2, 80, ROW)))
 SMALL = (*[(160, ROW)] * 2, (2, 80, ROW))
 BOX = (2, 5, 8, ROW)
-SENDS, RECVS, LOCALS, LAG = 70, 160, 28, 8
+SENDS, RECVS, LOCALS, LAG = 66, 160, 28, 9
 ORDER = (
     "A0 R0 O0 B0",
     "W0 A1 C0 R1",
-    "O1 W1 D0 B1",
-    "E0 C1 H0 D1",
-    "J0 E1 K0 H1",
-    "L0 Q0 J1 K1",
+    "O1 W1 D0 V0",
+    "B1 E0 C1 H0",
+    "D1 J0 V1 Y0",
+    "E1 K0 H1 L0",
+    "Q0 J1 Y1 K1",
     "M0 L1 Q1 N0",
     "M1 N1",
 )
@@ -236,8 +237,11 @@
             raw_phase(w, 1, k)
 
     def stage_d(k):
-        for w in range(3):
+        for w in range(2):
             meet(w, 1, k)
+
+    def stage_v(k):
+        meet(2, 1, k)
 
     def to_line(src, dst, *key):
         for t, device_id in zip(line, line_device):
@@ -331,6 +335,8 @@
 
         for w in range(2):
             open_whole(w, k)
+
+    def stage_y(k):
         arrived("g", 2, 2, k)
         open_whole(2, k)
 
@@ -376,7 +382,7 @@
 
     stages = {n[6:]: f for n, f in locals().items() if n.startswith("stage_")}
     for i, name in enumerate(" ".join(ORDER).lower().split()):
-        recycle(LAG if i < 27 else LAG // 2)
+        recycle(LAG if i < 31 else LAG // 2)
         stages[name[0]](int(name[1]))
 
     recycle(2)

time: 93.8 us -> 94.6 us (level)
  no operation moved by 1% of the time
where the time goes in v5:
time: 94.6 us; the launch traced here: 94.5 us
  Pallas kernels  93.8 us (99%)
    pallas_call x1, Pallas kernels, step(): pl.pallas_call(kernel, name='step', out_shape=[pltpu.VMEM(s, t) for s, t...  87.9 us
    pallas_call x1, Pallas kernels, step(): pl.pallas_call(write_out, name='write_out', out_shape=[jax.ShapeDtypeStru...  5.89 us

profile of v5, /device:TPU:1, one launch (start us, length us, event | category | flops | bytes accessed | tf_op | source)
XLA Modules:
  0.0 94.5 jit_solution(11094149748749359778)
XLA Ops:
  0.6 87.9 %step.1 = (bf16[2,4,4,5,2,64,128]{6,5,4,3,2,1,0:T(8,128)(2,1)S(1)}, bf16[2,4,4,5,2,64,128]{6,5,4,3,2,1,0:T(8,128)(2,1)S(1)}, bf16[2,4,4,4,2,80,128]{6,5,4,3,2,1,...) custom-call(bf16[2,4,4,5,2,64,128]{6,5,4,3,2,1,0:T(8,128)(2,1)} %bit, ...), custom_call_target="tpu_custom_call" | custom-call | tf_op jit(solution)/shard_map/step/pallas_call | solution.py:445
  88.6 5.9 %write_out.1 = (bf16[2,4,4,5,2,64,128]{6,5,4,3,2,1,0:T(8,128)(2,1)}, bf16[2,4,4,5,2,64,128]{6,5,4,3,2,1,0:T(8,128)(2,1)}, bf16[2,4,4,4,2,80,128]{6,5,4,3,2,1,0:T...) custom-call(bf16[2,4,4,5,2,64,128]{6,5,4,3,2,1,0:T(8,128)(2,1)S(1)} , ...), custom_call_target="tpu_custom_call" | custom-call | tf_op jit(solution)/shard_map/write_out/pallas_call | solution.py:465
